TPU v7x, 256 devices: a whole 4x4x8 slice. The times are simulated.
256 devices in a mesh: seq: 32 (over x, z), head: 8 (over y, core).
Axes of the slice: x: 4, y: 4, z: 8, core: 2. Of those that a mesh axis runs over, the one named last changes fastest.
Arguments:
- queries: bfloat16 [32, 64, 128], P('seq', 'head'), may hold values from -90 to 90
- keys: bfloat16 [32, 8, 16384, 128], P(None, 'head', 'seq'), may hold values from -4 to 4
- values: bfloat16 [32, 8, 16384, 128], P(None, 'head', 'seq'), may hold values from -6 to 6
- old_scores: float32 [32, 8, 16384], P(None, 'head', 'seq'), may hold values from 0 to 4
- lengths: int32 [32], replicated, may hold values from 4096 to 16384
- valid_counts: int32 [32, 128], P(None, 'seq'), may hold values from 1 to 128
Outputs:
- attended: bfloat16 [32, 64, 128], P('seq', 'head')
- heavy_scores: float32 [32, 8, 16384], P(None, 'head', 'seq')
Inputs may be any that keep to these rules, and one draw needn't show every extreme that they name: `lengths`: slot c of a sequence is cached when c is below its length. `valid_counts`: in block k of a sequence, the slots k * 128 + j with j below the count are live and the others are evicted.
All inputs are finite; a program needn't handle non-finite values.
Results may differ from a plain program's by a relative error of at most 0.0075.
Values may be sent and summed in bfloat16 or wider, within the bound.
A program may use at most 64 MiB of HBM per device.

v0:
```python
import jax
import jax.numpy as jnp
from jax import lax
from jax.sharding import PartitionSpec as P

HD = 128
BLK = 128


def copy_for_each(x, axis):
    copies = jnp.broadcast_to(x, (lax.axis_size(axis), *x.shape))
    return lax.all_to_all(copies, axis, split_axis=0, concat_axis=0, tiled=True)


def in_order(parts, dim):
    parts = jnp.moveaxis(parts, 0, dim)
    lengths = parts.shape
    return parts.reshape(*lengths[:dim], lengths[dim] * lengths[dim + 1], *lengths[dim + 2 :])


def gathered_copies(x, axis, dim):
    parts = copy_for_each(x, axis)
    return in_order(parts, dim)


def over_copies(x, axis):
    everything = copy_for_each(x, axis)
    return jnp.max(everything, axis=0)


def split_up(x, dim, count):
    lengths = x.shape
    parts = x.reshape(*lengths[:dim], count, lengths[dim] // count, *lengths[dim + 1 :])
    return jnp.moveaxis(parts, dim, 0)


def summed_on_arrival(x, axis, dim):
    parts = split_up(x, dim, lax.axis_size(axis))
    arrived = lax.all_to_all(parts, axis, split_axis=0, concat_axis=0, tiled=True)
    return arrived.sum(axis=0)


def side_by_side(arrays, axis, dim, along):
    columns = [a.reshape(*a.shape[:along], -1) for a in arrays]
    both = jnp.concatenate(columns, axis=along)
    filled, at, finished = (summed_on_arrival(both, axis, dim), 0, [])
    for a, column in zip(arrays, columns):
        share = filled[..., at : at + column.shape[along]]
        finished.append(share.reshape(*share.shape[:along], *a.shape[along:]))
        at += column.shape[along]
    return tuple(finished)


def on_device(queries, keys, values, old_scores, lengths, valid_counts):
    seq_dev = queries.shape[0]
    kv_local = keys.shape[1]
    ctx_dev = keys.shape[2]
    gathered = gathered_copies(queries, "seq", 0)
    seq_count = gathered.shape[0]
    group_size = gathered.shape[1] // kv_local
    grouped = gathered.reshape(seq_count, kv_local, group_size, HD)
    scores = jnp.einsum(
        "bhgd,bhcd->bhgc", grouped, keys, preferred_element_type=jnp.float32
    ) * HD ** (-0.5)
    offset = lax.axis_index("seq") * ctx_dev
    position = offset + jnp.arange(ctx_dev, dtype=jnp.int32)
    block_slot = jnp.arange(BLK, dtype=jnp.int32)
    in_block = (valid_counts[:, :, None] > block_slot[None, None, :]).reshape(seq_count, ctx_dev)
    live_mask = (position[None, :] < lengths[:, None]) & in_block
    masked = jnp.where(live_mask[:, None, None, :], scores, -jnp.inf)
    local_top = jnp.max(masked, axis=3)
    row_top = over_copies(local_top, "seq")
    exponent = jnp.exp(masked - row_top[:, :, :, None])
    weights = exponent.astype(jnp.bfloat16)
    partial_mixed = jnp.einsum(
        "bhgc,bhcd->bhgd", weights, values, preferred_element_type=jnp.float32
    )
    partial_total = jnp.sum(exponent, axis=3)
    own_mixed, own_total = side_by_side((partial_mixed, partial_total), "seq", 0, 3)
    row_total = gathered_copies(own_total, "seq", 0)
    heavy_scores = old_scores + jnp.sum(exponent / row_total[:, :, :, None], axis=2)
    attended = (own_mixed / own_total[:, :, :, None]).astype(jnp.bfloat16)
    attended = attended.reshape(seq_dev, kv_local * group_size, HD)
    return (attended, heavy_scores)


def solution(mesh):
    return jax.shard_map(
        on_device,
        mesh=mesh,
        in_specs=(
            P("seq", "head", None),
            P(None, "head", "seq", None),
            P(None, "head", "seq", None),
            P(None, "head", "seq"),
            P(),
            P(None, "seq"),
        ),
        out_specs=(P("seq", "head", None), P(None, "head", "seq")),
        check_vma=False,
    )
```

profile of v0, /device:TPU:8, one launch (start us, length us, event | category | flops | bytes accessed | tf_op | source)
XLA Modules:
  0.0 74.8 jit_solution(2132541103162587303)
XLA Ops:
  0.6 1.3 %broadcast_in_dim.28 = bf16[32,1,8,128]{3,2,1,0:T(8,128)(2,1)} broadcast(bf16[8,128]{1,0:T(8,128)(2,1)} %bitcast.47), dimensions={2,3} | broadcast | bytes 67584 | tf_op jit(solution)/shard_map/broadcast_in_dim | solution.py:11
  1.9 11.3 %all-to-all-start = ((bf16[32,1,8,128]{3,2,1,0:T(8,128)(2,1)}), bf16[32,1,8,128]{3,2,1,0:T(8,128)(2,1)S(1)}, u32[]{:S(2)}, u32[]{:S(2)}) async-start(bf16[32,1,8,128]{3,2,1,0:T(8,128)(2,1)} %broadcast_in_dim.28), calls=%async_computation | async-start | bytes 131072 | tf_op jit(solution)/shard_map/all_to_all | solution.py:12
  13.3 0.8 %copy.15 = s32[32,4]{1,0:T(8,128)S(1)} copy(s32[32,4]{0,1:T(4,128)} %param.11) | data formatting | bytes 1024 | tf_op args[5]
  14.1 0.1 gt.24
  14.2 0.7 fusion.18
  14.9 8.4 %all-to-all-done = bf16[32,1,8,128]{3,2,1,0:T(8,128)(2,1)S(1)} async-done(((bf16[32,1,8,128]{3,2,1,0:T(8,128)(2,1)}), bf16[32,1,8,128]{3,2,1,0:T(8,128)(2,1)S(1)}, u32[]{:S(2)}, u32[]{:S(2)}) %all-to-all-start) | async-done | bytes 65568 | tf_op jit(solution)/shard_map/all_to_all | solution.py:12
  23.3 3.5 %fusion.21 = (f32[32,8]{1,0:T(8,128)S(1)}, f32[32,8,512]{2,1,0:T(8,128)S(1)}) fusion(bf16[32,1,512,128]{3,2,1,0:T(8,128)(2,1)} %param.7, bf16[32,1,8,128]{3,2,1,0:T(8,128)(2,1)S(1)} %all-to-all-done, pred[32,512]{1,0:T(8,128)(4,1)S(1)} %fusion.18), kind=kOutput, calls=%fused_computation.23 | convolution fusion | flops 33947392 | bytes 4801536 | tf_op jit(solution)/shard_map/bhgd,bhcd->bhgc/dot_general | solution.py:62
  26.7 0.0 copy-start
  26.7 0.1 copy.16
  26.8 0.1 reshape.112
  27.0 13.1 %all_to_all.20 = f32[32,1,256]{2,1,0:T(1,128)S(1)} all-to-all(f32[32,1,256]{2,1,0:T(1,128)S(1)} %reshape.112), channel_id=1, replica_groups=mesh['seq'=32,'head'=8] {'seq'}, dimensions={0} | all-to-all | bytes 65536 | tf_op jit(solution)/shard_map/all_to_all | solution.py:12
  40.0 0.5 broadcast.44
  40.5 0.7 reduce.10
  41.3 0.1 reshape.113
  41.4 0.1 copy.17
  41.5 0.2 fusion.13
  41.7 0.3 copy.19
  41.9 2.9 %fusion.10 = f32[32,1,8,128]{3,2,0,1:T(8,128)S(1)} fusion(bf16[32,1,512,128]{3,2,1,0:T(8,128)(2,1)} %param.8, f32[32,8,512]{2,1,0:T(8,128)S(1)} %get-tuple-element.3, f32[32,8]{1,0:T(8,128)S(1)} %copy.17), kind=kOutput, calls=%fused_computation.6 | convolution fusion | flops 33816576 | bytes 4850688 | tf_op jit(solution)/shard_map/bhgc,bhcd->bhgd/dot_general | solution.py:75
  44.9 13.9 %all_to_all.21 = f32[32,1,1,8,129]{4,3,2,1,0:T(8,128)S(1)} all-to-all(f32[32,1,1,8,129]{4,3,2,1,0:T(8,128)S(1)} %maximum_bitcast_fusion), channel_id=1, replica_groups=mesh['seq'=32,'head'=8] {'seq'}, dimensions={0} | all-to-all | bytes 264192 | tf_op jit(solution)/shard_map/all_to_all | solution.py:39
  58.9 0.1 slice_reduce_fusion
  59.0 0.6 broadcast_in_dim.31
  59.6 4.5 %all-to-all-start.3 = ((f32[32,1,1,8]{3,2,1,0:T(1,128)}), f32[32,1,1,8]{3,2,1,0:T(1,128)S(1)}, u32[]{:S(2)}, u32[]{:S(2)}) async-start(f32[32,1,1,8]{3,2,1,0:T(1,128)} %broadcast_in_dim.31), calls=%async_computation.3 | async-start | bytes 32768 | tf_op jit(solution)/shard_map/all_to_all | solution.py:12
  64.1 0.7 fusion.20
  64.8 9.1 %all-to-all-done.3 = f32[32,1,1,8]{3,2,1,0:T(1,128)S(1)} async-done(((f32[32,1,1,8]{3,2,1,0:T(1,128)}), f32[32,1,1,8]{3,2,1,0:T(1,128)S(1)}, u32[]{:S(2)}, u32[]{:S(2)}) %all-to-all-start.3) | async-done | bytes 1056 | tf_op jit(solution)/shard_map/all_to_all | solution.py:12
  73.9 0.3 divide_reduce_fusion
  74.1 0.0 copy-done
  74.1 0.7 reshape_add_fusion
  (6 shorter events, 0.1 us)
Async XLA Ops:
  1.9 21.3 %all-to-all-start = ((bf16[32,1,8,128]{3,2,1,0:T(8,128)(2,1)}), bf16[32,1,8,128]{3,2,1,0:T(8,128)(2,1)S(1)}, u32[]{:S(2)}, u32[]{:S(2)}) async-start(bf16[32,1,8,128]{3,2,1,0:T(8,128)(2,1)} %broadcast_in_dim.28), calls=%async_computation | async-start | bytes 131072 | tf_op jit(solution)/shard_map/all_to_all | solution.py:12
  26.7 47.4 %copy-start = (f32[32,1,512]{2,1,0:T(1,128)S(1)}, f32[32,1,512]{2,1,0:T(1,128)}, u32[]{:S(2)}) copy-start(f32[32,1,512]{2,1,0:T(1,128)} %param.9) | copy-start | bytes 196612
  59.6 14.2 %all-to-all-start.3 = ((f32[32,1,1,8]{3,2,1,0:T(1,128)}), f32[32,1,1,8]{3,2,1,0:T(1,128)S(1)}, u32[]{:S(2)}, u32[]{:S(2)}) async-start(f32[32,1,1,8]{3,2,1,0:T(1,128)} %broadcast_in_dim.31), calls=%async_computation.3 | async-start | bytes 32768 | tf_op jit(solution)/shard_map/all_to_all | solution.py:12
where the time goes:
time: 75.3 us; the launch traced here: 74.8 us
  blocking collectives  27 us (36%)
  waiting for transfers between devices  17.5 us (23%)
  starting transfers between devices  15.8 us (21%)
  matrix products  6.35 us (8%)
  local copies, waits for them, and re-layouts  4.05 us (5%)
  other arithmetic  3.43 us (5%)
    all_to_all x2, waiting for transfers between devices, copy_for_each(): return lax.all_to_all(copies, axis, split_axis=0, concat_axis=0, tiled=True)  17.5 us
    all_to_all x2, starting transfers between devices, copy_for_each(): return lax.all_to_all(copies, axis, split_axis=0, concat_axis=0, tiled=True)  15.8 us
    all_to_all x1, blocking collectives, summed_on_arrival(): lax.all_to_all(parts, axis, split_axis=0, concat_axis=0, tiled=True)  13.9 us
    all_to_all x1, blocking collectives, copy_for_each(): return lax.all_to_all(copies, axis, split_axis=0, concat_axis=0, tiled=True)  13.1 us
    dot_general x1, matrix products, on_device(): jnp.einsum('bhgd,bhcd->bhgc', grouped, keys, preferred_element_type=jnp.f...  3.45 us
    dot_general x1, matrix products, on_device(): jnp.einsum('bhgc,bhcd->bhgd', weights, values, preferred_element_type=jnp...  2.89 us
    broadcast_in_dim x2, local copies, waits for them, and re-layouts, copy_for_each(): copies = jnp.broadcast_to(x, (lax.axis_size(axis), *x.shape))  1.94 us
  transfers between devices with their start and end apart: 2, of which 2 were waited for; matrix products, arithmetic and copies ran while one was open for 3% of the time, Pallas kernels for 0%

commit v1 on v0

v1 whole, which is shorter than its diff:
```python
import functools

import jax
import jax.numpy as jnp
from jax import lax
from jax.experimental import pallas as pl
from jax.experimental.pallas import tpu as pltpu
from jax.sharding import PartitionSpec as P

HD = 128
BLK = 128
NX, NZ = 4, 8
NEG = -1e30
FLOOR = -1e29
TINY = 1e-30
MESH = pl.DeviceIdType.MESH


def zigzag(k):
    return ((k + 1) // 2) * (2 * (k % 2) - 1)


def kernel(
    n, heads, ctx, q_hbm, k_hbm, v_hbm, len_hbm, val_hbm, con_ref, att_ref,
    kbuf, vbuf, qbuf, obuf, mixbuf, pbuf, stat, statall, ltot, len_s, val_s,
    ksem, vsem, lsem, qsend, qrecv, osend, orecv, ssend, srecv,
):
    me = lax.axis_index("seq")
    mx, mz = me // NZ, me % NZ
    blocks = ctx // BLK
    half = n // 2

    def peer_at(i):
        dx = NX // 2 + zigzag(i % NX)
        dz = NZ // 2 + zigzag(i // NX)
        return ((mx + dx) % NX) * NZ + (mz + dz) % NZ

    barrier = pltpu.get_barrier_semaphore()

    def greet(i, _):
        pl.semaphore_signal(barrier, inc=1, device_id={"seq": peer_at(i)}, device_id_type=MESH)
        return 0

    lax.fori_loop(0, n - 1, greet, 0, unroll=True)

    q_load = pltpu.make_async_copy(q_hbm.at[0], qbuf.at[me], lsem.at[0])
    len_load = pltpu.make_async_copy(len_hbm, len_s, lsem.at[1])
    val_load = pltpu.make_async_copy(val_hbm, val_s, lsem.at[2])
    q_load.start()
    len_load.start()
    val_load.start()
    loads = []
    for c in range(4):
        rows = pl.ds(c * (n // 4), n // 4)
        loads.append(pltpu.make_async_copy(k_hbm.at[rows, 0], kbuf.at[rows], ksem.at[c]))
        loads.append(pltpu.make_async_copy(v_hbm.at[rows, 0], vbuf.at[rows], vsem.at[c]))
    for load in loads:
        load.start()
    q_load.wait()
    pl.semaphore_wait(barrier, n - 1)

    def q_copy(slot, peer):
        return pltpu.make_async_remote_copy(
            src_ref=qbuf.at[me], dst_ref=qbuf.at[slot], send_sem=qsend.at[peer], recv_sem=qrecv.at[slot],
            device_id={"seq": peer}, device_id_type=MESH,
        )

    def o_copy(b, slot):
        return pltpu.make_async_remote_copy(
            src_ref=obuf.at[b], dst_ref=mixbuf.at[slot], send_sem=osend.at[b], recv_sem=orecv.at[slot],
            device_id={"seq": b}, device_id_type=MESH,
        )

    def s_copy(slot, peer):
        return pltpu.make_async_remote_copy(
            src_ref=stat, dst_ref=statall.at[slot], send_sem=ssend.at[peer], recv_sem=srecv.at[slot],
            device_id={"seq": peer}, device_id_type=MESH,
        )

    def send_q(i, _):
        q_copy(me, peer_at(i)).start()
        return 0

    lax.fori_loop(0, n - 1, send_q, 0, unroll=True)
    len_load.wait()
    val_load.wait()
    for load in loads:
        load.wait()

    base = me * ctx
    row2 = lax.broadcasted_iota(jnp.int32, (2 * heads, BLK), 0)
    lane2 = lax.broadcasted_iota(jnp.int32, (2 * heads, BLK), 1)
    upper = row2 < heads
    skew = (
        lax.broadcasted_iota(jnp.int32, (heads, BLK), 1)
        - lax.broadcasted_iota(jnp.int32, (heads, BLK), 0)
    )

    def scores_of(pair):
        b0 = 2 * pair
        qp = qbuf[pl.ds(b0, 2)].astype(jnp.float32).reshape(2 * heads, HD)
        lhs = jnp.concatenate([jnp.where(upper, qp, 0.0), jnp.where(upper, 0.0, qp)], axis=1).astype(jnp.bfloat16)
        keys = jnp.concatenate([kbuf[b0], kbuf[b0 + 1]], axis=1)
        s = lax.dot_general(lhs, keys, (((1,), (1,)), ((), ())), preferred_element_type=jnp.float32)
        s = s * HD ** (-0.5)
        parts = []
        for j in range(blocks):
            lim = [jnp.minimum(val_s[j, b0 + r], len_s[b0 + r] - base - j * BLK) for r in range(2)]
            limit = jnp.where(upper, lim[0], lim[1])
            parts.append(jnp.where(lane2 < limit, s[:, j * BLK : (j + 1) * BLK], NEG))
        return parts

    def tree(op, parts):
        while len(parts) > 1:
            parts = [op(parts[i], parts[i + 1]) for i in range(0, len(parts), 2)]
        return parts[0]

    def group(gi, carry):
        l0, l1, m0, m1 = carry
        zo = (mz // 2 + zigzag(gi)) % (NZ // 2)
        pairs = [((mx + xo) % NX) * (NZ // 2) + zo for xo in (0, 1, 3, 2)]
        for pair in pairs:
            for r in range(2):
                b = 2 * pair + r

                @pl.when(b != me)
                def _():
                    q_copy(b, b).wait_recv()

        parts = [scores_of(pair) for pair in pairs]
        tops = [
            jnp.maximum(jnp.max(tree(jnp.maximum, ps), axis=1, keepdims=True), FLOOR) for ps in parts
        ]
        expos = [[jnp.exp(s - top) for s in ps] for ps, top in zip(parts, tops)]
        totals = [
            jnp.maximum(jnp.sum(tree(jnp.add, es), axis=1, keepdims=True), TINY) for es in expos
        ]
        for pair, top, es, total in zip(pairs, tops, expos, totals):
            b0 = 2 * pair
            w = jnp.concatenate(es, axis=1).astype(jnp.bfloat16)
            pbuf[pl.ds(pl.multiple_of(pair * 2 * heads, 2 * heads), 2 * heads), :] = w
            vals = jnp.concatenate([vbuf[b0], vbuf[b0 + 1]], axis=1)
            mixed = jnp.dot(w, vals, preferred_element_type=jnp.float32)
            inv = 1.0 / total
            lse = top + jnp.log(total)
            for r in range(2):
                rows = slice(r * heads, (r + 1) * heads)
                part = mixed[rows, r * HD : (r + 1) * HD] * inv[rows]
                obuf[b0 + r] = part.astype(jnp.bfloat16)
                at = (b0 + r) * heads
                l0 = jnp.where(skew == at, lse[rows], l0)
                l1 = jnp.where(skew == at - BLK, lse[rows], l1)
                m0 = jnp.where(skew == at, top[rows], m0)
                m1 = jnp.where(skew == at - BLK, top[rows], m1)
        for pair in pairs:
            for r in range(2):
                b = 2 * pair + r

                @pl.when(b != me)
                def _():
                    o_copy(b, me).start()

        return l0, l1, m0, m1

    zero = jnp.zeros((heads, BLK), jnp.float32)
    l0, l1, m0, m1 = lax.fori_loop(0, NZ // 2, group, (zero, zero, zero, zero))

    own = jnp.concatenate([jnp.sum(l0, axis=0, keepdims=True), jnp.sum(l1, axis=0, keepdims=True)], axis=0)
    tops = jnp.concatenate([jnp.sum(m0, axis=0, keepdims=True), jnp.sum(m1, axis=0, keepdims=True)], axis=0)
    stat[...] = own
    statall[me] = own

    def send_s(i, _):
        s_copy(me, peer_at(i)).start()
        return 0

    lax.fori_loop(0, n - 1, send_s, 0, unroll=True)
    mixbuf[me] = obuf[me]

    def take_s(i, _):
        src = peer_at(n - 2 - i)
        s_copy(src, src).wait_recv()
        return 0

    lax.fori_loop(0, n - 1, take_s, 0, unroll=True)

    every = statall[...]
    top = jnp.max(every, axis=0)
    lse = top + jnp.log(jnp.sum(jnp.exp(every - top[None]), axis=0))
    ltot[...] = lse
    share = jnp.exp(tops - lse)
    rows_h = lax.broadcasted_iota(jnp.int32, (half, BLK), 0)
    lanes_h = lax.broadcasted_iota(jnp.int32, (half, BLK), 1) // heads
    for r in range(2):
        spread = jnp.where(rows_h == lanes_h, jnp.broadcast_to(share[r : r + 1], (half, BLK)), 0.0)
        high = spread.astype(jnp.bfloat16)
        low = (spread - high.astype(jnp.float32)).astype(jnp.bfloat16)
        both = jnp.concatenate([high, low], axis=0)
        got = jnp.dot(both, pbuf[r * BLK : (r + 1) * BLK, :], preferred_element_type=jnp.float32)
        con_ref[r * half : (r + 1) * half, :] = got[:half] + got[half:]

    def take_o(i, _):
        src = peer_at(n - 2 - i)
        o_copy(src, src).wait_recv()
        return 0

    lax.fori_loop(0, n - 1, take_o, 0, unroll=True)

    my_row = me // half
    hit = skew == (me % half) * heads
    total_row = ltot[pl.ds(my_row, 1), :]
    acc = zero
    for d in range(n):
        gap = jnp.broadcast_to(statall[d, pl.ds(my_row, 1), :] - total_row, (heads, BLK))
        part = jnp.exp(jnp.sum(jnp.where(hit, gap, 0.0), axis=1, keepdims=True))
        acc = acc + part * mixbuf[d].astype(jnp.float32)
    att_ref[...] = acc

    def finish(i, _):
        peer = peer_at(i)
        q_copy(me, peer).wait_send()
        o_copy(peer, me).wait_send()
        s_copy(me, peer).wait_send()
        return 0

    lax.fori_loop(0, n - 1, finish, 0, unroll=True)


def on_device(queries, keys, values, old_scores, lengths, valid_counts):
    n = lax.axis_size("seq")
    heads = queries.shape[1]
    ctx = keys.shape[2]
    blocks = ctx // BLK
    anywhere = pl.BlockSpec(memory_space=pl.ANY)
    vmem = pl.BlockSpec(memory_space=pltpu.VMEM)
    dma = pltpu.SemaphoreType.DMA
    added, attended = pl.pallas_call(
        functools.partial(kernel, n, heads, ctx),
        out_shape=(
            jax.ShapeDtypeStruct((n, ctx), jnp.float32),
            jax.ShapeDtypeStruct((heads, HD), jnp.float32),
        ),
        in_specs=[anywhere] * 5,
        out_specs=(vmem, vmem),
        scratch_shapes=[
            pltpu.VMEM((n, ctx, HD), jnp.bfloat16),
            pltpu.VMEM((n, ctx, HD), jnp.bfloat16),
            pltpu.VMEM((n, heads, HD), jnp.bfloat16),
            pltpu.VMEM((n, heads, HD), jnp.bfloat16),
            pltpu.VMEM((n, heads, HD), jnp.bfloat16),
            pltpu.VMEM((n * heads, ctx), jnp.bfloat16),
            pltpu.VMEM((2, BLK), jnp.float32),
            pltpu.VMEM((n, 2, BLK), jnp.float32),
            pltpu.VMEM((2, BLK), jnp.float32),
            pltpu.SMEM((n,), jnp.int32),
            pltpu.SMEM((blocks, n), jnp.int32),
            dma((4,)),
            dma((4,)),
            dma((3,)),
            dma((n,)),
            dma((n,)),
            dma((n,)),
            dma((n,)),
            dma((n,)),
            dma((n,)),
        ],
        compiler_params=pltpu.CompilerParams(collective_id=0, has_side_effects=True),
        name="decode",
    )(queries, keys, values, lengths, valid_counts.T)
    heavy = old_scores + added.reshape(old_scores.shape)
    return attended.astype(jnp.bfloat16)[None], heavy


def solution(mesh):
    return jax.shard_map(
        on_device,
        mesh=mesh,
        in_specs=(
            P("seq", "head", None),
            P(None, "head", "seq", None),
            P(None, "head", "seq", None),
            P(None, "head", "seq"),
            P(),
            P(None, "seq"),
        ),
        out_specs=(P("seq", "head", None), P(None, "head", "seq")),
        check_vma=False,
    )
```

time: 75.3 us -> 28.9 us (0.38)
  blocking collectives: 27 us -> 0 us
  Pallas kernels: 0 us -> 25.3 us
  waiting for transfers between devices: 17.5 us -> 0 us
  starting transfers between devices: 15.8 us -> 0 us
  matrix products: 6.35 us -> 0 us
  local copies, waits for them, and re-layouts: 4.05 us -> 0.7 us
  other arithmetic: 3.43 us -> 2.11 us
    all_to_all x2 -> x0, blocking collectives: 27 us -> none  [the longest x1 13.9 us: summed_on_arrival(): lax.all_to_all(parts, axis, split_axis=0, concat_axis=0, tiled=True)]
    pallas_call x0 -> x1, Pallas kernels: none -> 25.3 us  [on_device(): pl.pallas_call(functools.partial(kernel, n, heads, ctx), out_shape=(jax.S...]
    all_to_all x2 -> x0, waiting for transfers between devices: 17.5 us -> none  [copy_for_each(): return lax.all_to_all(copies, axis, split_axis=0, concat_axis=0, tiled=True)]
    all_to_all x2 -> x0, starting transfers between devices: 15.8 us -> none  [copy_for_each(): return lax.all_to_all(copies, axis, split_axis=0, concat_axis=0, tiled=True)]
    dot_general x2 -> x0, matrix products: 6.35 us -> none  [the longest x1 3.45 us: on_device(): jnp.einsum('bhgd,bhcd->bhgc', grouped, keys, preferred_element_type=jnp.f...]
    broadcast_in_dim x2 -> x0, local copies, waits for them, and re-layouts: 1.94 us -> none  [copy_for_each(): copies = jnp.broadcast_to(x, (lax.axis_size(axis), *x.shape))]
    broadcast_in_dim x0 -> x1, other arithmetic: none -> 1.26 us  [on_device(): return (attended.astype(jnp.bfloat16)[None], heavy)]
  transfers between devices with their start and end apart: 2 -> 0, of which waited for: 2 -> 0; matrix products, arithmetic and copies ran while one was open for 3% -> 0% of each run, Pallas kernels for 0% -> 0%
where the time goes in v1:
time: 28.9 us; the launch traced here: 28.8 us
  Pallas kernels  25.3 us (88%)
  other arithmetic  2.11 us (7%)
  local copies, waits for them, and re-layouts  0.7 us (2%)
  between operations  0.65 us (2%)
    pallas_call x1, Pallas kernels, on_device(): pl.pallas_call(functools.partial(kernel, n, heads, ctx), out_shape=(jax.S...  25.3 us
    broadcast_in_dim x1, other arithmetic, on_device(): return (attended.astype(jnp.bfloat16)[None], heavy)  1.26 us
    add x1, other arithmetic, on_device(): heavy = old_scores + added.reshape(old_scores.shape)  0.85 us
    unnamed x3, local copies, waits for them, and re-layouts  0.7 us

profile of v1, /device:TPU:8, one launch (start us, length us, event | category | flops | bytes accessed | tf_op | source)
XLA Modules:
  0.0 28.8 jit_solution(6271811962234520259)
XLA Ops:
  0.6 0.0 copy-start
  0.6 25.3 %decode.1 = (f32[32,512]{1,0:T(8,128)}, f32[8,128]{1,0:T(8,128)}) custom-call(bf16[1,8,128]{2,1,0:T(8,128)(2,1)} %q_hbm.1, bf16[32,1,512,128]{3,2,1,0:T(8,128)(2,1)} %k_hbm.1, bf16[32,1,512,128]{3,2,1,0:T(8,128)(2,1)} %v_hbm.1, s32[32]{0:T(128)} %len_hbm.1, s32[4,32]{1,0:T(4,128)} %bitcast.5), custom_call_target="tpu_custom_call" | custom-call | tf_op jit(solution)/shard_map/decode/pallas_call | solution.py:237
  26.0 1.3 %convert_bitcast_fusion = bf16[1,8,128]{2,1,0:T(8,128)(2,1)} fusion(f32[8,128]{1,0:T(8,128)} %get-tuple-element.4), kind=kLoop, calls=%fused_computation.1 | loop fusion | flops 1024 | bytes 6144 | tf_op jit(solution)/shard_map/broadcast_in_dim | solution.py:271
  27.2 0.0 copy-done
  27.2 0.8 %bitcast_add_fusion = f32[32,1,512]{2,0,1:T(8,128)S(1)} fusion(f32[32,512]{1,0:T(8,128)} %get-tuple-element.5, f32[32,1,512]{2,1,0:T(1,128)S(1)} %copy-done), kind=kLoop, calls=%fused_computation | loop fusion | flops 16384 | bytes 196608 | tf_op jit(solution)/shard_map/add | solution.py:270
  28.1 0.7 %copy.9 = f32[32,1,512]{2,1,0:T(1,128)} copy(f32[32,1,512]{2,0,1:T(8,128)S(1)} %bitcast_add_fusion) | data formatting | bytes 131072
Async XLA Ops:
  0.6 26.6 %copy-start = (f32[32,1,512]{2,1,0:T(1,128)S(1)}, f32[32,1,512]{2,1,0:T(1,128)}, u32[]{:S(2)}) copy-start(f32[32,1,512]{2,1,0:T(1,128)} %param.9) | copy-start | bytes 196612

commit v2 on v1

--- a/solution.py
+++ b/solution.py
@@ -22,7 +22,7 @@
 
 def kernel(
     n, heads, ctx, q_hbm, k_hbm, v_hbm, len_hbm, val_hbm, con_ref, att_ref,
-    kbuf, vbuf, qbuf, obuf, mixbuf, pbuf, stat, statall, ltot, len_s, val_s,
+    kbuf, vbuf, kturn, qbuf, obuf, mixbuf, pbuf, stat, statall, ltot, len_s, val_s,
     ksem, vsem, lsem, qsend, qrecv, osend, orecv, ssend, srecv,
 ):
     me = lax.axis_index("seq")
@@ -87,6 +87,12 @@
     for load in loads:
         load.wait()
 
+    def turn(b, _):
+        kturn[b] = kbuf[b].T
+        return 0
+
+    lax.fori_loop(0, n, turn, 0, unroll=4)
+
     base = me * ctx
     row2 = lax.broadcasted_iota(jnp.int32, (2 * heads, BLK), 0)
     lane2 = lax.broadcasted_iota(jnp.int32, (2 * heads, BLK), 1)
@@ -100,8 +106,8 @@
         b0 = 2 * pair
         qp = qbuf[pl.ds(b0, 2)].astype(jnp.float32).reshape(2 * heads, HD)
         lhs = jnp.concatenate([jnp.where(upper, qp, 0.0), jnp.where(upper, 0.0, qp)], axis=1).astype(jnp.bfloat16)
-        keys = jnp.concatenate([kbuf[b0], kbuf[b0 + 1]], axis=1)
-        s = lax.dot_general(lhs, keys, (((1,), (1,)), ((), ())), preferred_element_type=jnp.float32)
+        keys = jnp.concatenate([kturn[b0], kturn[b0 + 1]], axis=0)
+        s = jnp.dot(lhs, keys, preferred_element_type=jnp.float32)
         s = s * HD ** (-0.5)
         parts = []
         for j in range(blocks):
@@ -197,7 +203,9 @@
         low = (spread - high.astype(jnp.float32)).astype(jnp.bfloat16)
         both = jnp.concatenate([high, low], axis=0)
         got = jnp.dot(both, pbuf[r * BLK : (r + 1) * BLK, :], preferred_element_type=jnp.float32)
-        con_ref[r * half : (r + 1) * half, :] = got[:half] + got[half:]
+        got = got[:half] + got[half:]
+        for j in range(blocks):
+            con_ref[pl.ds(r * half * blocks + j, half, stride=blocks), :] = got[:, j * BLK : (j + 1) * BLK]
 
     def take_o(i, _):
         src = peer_at(n - 2 - i)
@@ -226,18 +234,23 @@
     lax.fori_loop(0, n - 1, finish, 0, unroll=True)
 
 
+def closing(con_ref, att_ref, old_ref, attended_ref, heavy_ref):
+    attended_ref[...] = att_ref[...].astype(jnp.bfloat16)
+    heavy_ref[...] = old_ref[...] + con_ref[...]
+
+
 def on_device(queries, keys, values, old_scores, lengths, valid_counts):
     n = lax.axis_size("seq")
     heads = queries.shape[1]
     ctx = keys.shape[2]
     blocks = ctx // BLK
-    anywhere = pl.BlockSpec(memory_space=pl.ANY)
+    anywhere = pl.BlockSpec(memory_space=pltpu.HBM)
     vmem = pl.BlockSpec(memory_space=pltpu.VMEM)
     dma = pltpu.SemaphoreType.DMA
     added, attended = pl.pallas_call(
         functools.partial(kernel, n, heads, ctx),
         out_shape=(
-            jax.ShapeDtypeStruct((n, ctx), jnp.float32),
+            jax.ShapeDtypeStruct((n * blocks, BLK), jnp.float32),
             jax.ShapeDtypeStruct((heads, HD), jnp.float32),
         ),
         in_specs=[anywhere] * 5,
@@ -245,6 +258,7 @@
         scratch_shapes=[
             pltpu.VMEM((n, ctx, HD), jnp.bfloat16),
             pltpu.VMEM((n, ctx, HD), jnp.bfloat16),
+            pltpu.VMEM((n, HD, ctx), jnp.bfloat16),
             pltpu.VMEM((n, heads, HD), jnp.bfloat16),
             pltpu.VMEM((n, heads, HD), jnp.bfloat16),
             pltpu.VMEM((n, heads, HD), jnp.bfloat16),
@@ -264,11 +278,23 @@
             dma((n,)),
             dma((n,)),
         ],
-        compiler_params=pltpu.CompilerParams(collective_id=0, has_side_effects=True),
+        compiler_params=pltpu.CompilerParams(
+            collective_id=0, has_side_effects=True, vmem_limit_bytes=16 * 2**20
+        ),
         name="decode",
-    )(queries, keys, values, lengths, valid_counts.T)
-    heavy = old_scores + added.reshape(old_scores.shape)
-    return attended.astype(jnp.bfloat16)[None], heavy
+    )(*(pltpu.with_memory_space_constraint(a, pltpu.HBM) for a in (queries, keys, values, lengths, valid_counts.T)))
+    attended, heavy = pl.pallas_call(
+        closing,
+        out_shape=(
+            jax.ShapeDtypeStruct((heads, HD), jnp.bfloat16),
+            jax.ShapeDtypeStruct((n * blocks, BLK), jnp.float32),
+        ),
+        in_specs=[vmem] * 3,
+        out_specs=(vmem, vmem),
+        compiler_params=pltpu.CompilerParams(vmem_limit_bytes=2**20),
+        name="closing",
+    )(added, attended, old_scores.reshape(n * blocks, BLK))
+    return attended[None], heavy.reshape(old_scores.shape)
 
 
 def solution(mesh):

time: 28.9 us -> 25.8 us (0.89)
  other arithmetic: 2.11 us -> 0 us
  local copies, waits for them, and re-layouts: 0.7 us -> 0.01 us
  Pallas kernels: 25.3 us -> 25 us
    broadcast_in_dim x1 -> x0, other arithmetic: 1.26 us -> none  [on_device(): return (attended.astype(jnp.bfloat16)[None], heavy)]
    pallas_call x1, Pallas kernels: 25.3 us -> 24.4 us  [on_device(): pl.pallas_call(functools.partial(kernel, n, heads, ctx), out_shape=(jax.S...]
    add x1 -> x0, other arithmetic: 0.85 us -> none  [on_device(): heavy = old_scores + added.reshape(old_scores.shape)]
    unnamed x3 -> x2, local copies, waits for them, and re-layouts: 0.7 us -> 0.01 us
    pallas_call x0 -> x1, Pallas kernels: none -> 0.64 us  [on_device(): pl.pallas_call(closing, out_shape=(jax.ShapeDtypeStruct((heads, HD), jnp....]
where the time goes in v2:
time: 25.8 us; the launch traced here: 25.7 us
  Pallas kernels  25 us (97%)
  between operations  0.66 us (3%)
    pallas_call x1, Pallas kernels, on_device(): pl.pallas_call(functools.partial(kernel, n, heads, ctx), out_shape=(jax.S...  24.4 us
    pallas_call x1, Pallas kernels, on_device(): pl.pallas_call(closing, out_shape=(jax.ShapeDtypeStruct((heads, HD), jnp....  0.64 us

profile of v2, /device:TPU:8, one launch (start us, length us, event | category | flops | bytes accessed | tf_op | source)
XLA Modules:
  0.0 25.7 jit_solution(9833950687763357992)
XLA Ops:
  0.6 0.0 copy-start
  0.6 24.4 %decode.1 = (f32[128,128]{1,0:T(8,128)S(1)}, f32[8,128]{1,0:T(8,128)S(1)}) custom-call(bf16[1,8,128]{2,1,0:T(8,128)(2,1)} %q_hbm.1, bf16[32,1,512,128]{3,2,1,0:T(8,128)(2,1)} %k_hbm.1, bf16[32,1,512,128]{3,2,1,0:T(8,128)(2,1)} %v_hbm.1, s32[32]{0:T(128)} %len_hbm.1, s32[4,32]{1,0:T(4,128)} %bitcast.5), custom_call_target="tpu_custom_call" | custom-call | tf_op jit(solution)/shard_map/decode/pallas_call | solution.py:250
  25.0 0.0 copy-done
  25.0 0.6 %closing.1 = (bf16[8,128]{1,0:T(8,128)(2,1)}, f32[128,128]{1,0:T(8,128)}) custom-call(f32[128,128]{1,0:T(8,128)S(1)} %get-tuple-element.6.con_ref, f32[8,128]{1,0:T(8,128)S(1)} %get-tuple-element.7.att_ref, f32[128,128]{1,0:T(8,128)S(1)} %bitcast.4), custom_call_target="tpu_custom_call" | custom-call | tf_op jit(solution)/shard_map/closing/pallas_call | solution.py:286
Async XLA Ops:
  0.6 24.4 %copy-start = (f32[32,1,512]{2,1,0:T(1,128)S(1)}, f32[32,1,512]{2,1,0:T(1,128)}, u32[]{:S(2)}) copy-start(f32[32,1,512]{2,1,0:T(1,128)} %param.9) | copy-start | bytes 196612

commit v3 on v2

--- a/solution.py
+++ b/solution.py
@@ -30,18 +30,24 @@
     blocks = ctx // BLK
     half = n // 2
 
-    def peer_at(i):
-        dx = NX // 2 + zigzag(i % NX)
-        dz = NZ // 2 + zigzag(i // NX)
-        return ((mx + dx) % NX) * NZ + (mz + dz) % NZ
+    def pairs_of(k):
+        zo = (mz // 2 + zigzag(k)) % (NZ // 2)
+        return [((mx + xo) % NX) * (NZ // 2) + zo for xo in (0, 1, 3, 2)]
+
+    def peers_of(k):
+        found = []
+        for pair in pairs_of(k)[::-1]:
+            found += [2 * pair, 2 * pair + 1]
+        return found[:-2] + [me + 1 - 2 * (me % 2)] if k == 0 else found
+
+    groups = NZ // 2
+    far_first = list(range(groups))[::-1]
+    seen_as = (0, 2, 1, 3)
 
     barrier = pltpu.get_barrier_semaphore()
-
-    def greet(i, _):
-        pl.semaphore_signal(barrier, inc=1, device_id={"seq": peer_at(i)}, device_id_type=MESH)
-        return 0
-
-    lax.fori_loop(0, n - 1, greet, 0, unroll=True)
+    for k in far_first:
+        for peer in peers_of(k):
+            pl.semaphore_signal(barrier, inc=1, device_id={"seq": peer}, device_id_type=MESH)
 
     q_load = pltpu.make_async_copy(q_hbm.at[0], qbuf.at[me], lsem.at[0])
     len_load = pltpu.make_async_copy(len_hbm, len_s, lsem.at[1])
@@ -59,29 +65,31 @@
     q_load.wait()
     pl.semaphore_wait(barrier, n - 1)
 
-    def q_copy(slot, peer):
+    def q_copy(peer, k):
         return pltpu.make_async_remote_copy(
-            src_ref=qbuf.at[me], dst_ref=qbuf.at[slot], send_sem=qsend.at[peer], recv_sem=qrecv.at[slot],
+            src_ref=qbuf.at[me], dst_ref=qbuf.at[me], send_sem=qsend, recv_sem=qrecv.at[seen_as[k]],
             device_id={"seq": peer}, device_id_type=MESH,
         )
 
-    def o_copy(b, slot):
+    def o_copy(b):
         return pltpu.make_async_remote_copy(
-            src_ref=obuf.at[b], dst_ref=mixbuf.at[slot], send_sem=osend.at[b], recv_sem=orecv.at[slot],
+            src_ref=obuf.at[b], dst_ref=mixbuf.at[me], send_sem=osend, recv_sem=orecv,
             device_id={"seq": b}, device_id_type=MESH,
         )
 
-    def s_copy(slot, peer):
+    def s_copy(peer):
         return pltpu.make_async_remote_copy(
-            src_ref=stat, dst_ref=statall.at[slot], send_sem=ssend.at[peer], recv_sem=srecv.at[slot],
+            src_ref=stat, dst_ref=statall.at[me], send_sem=ssend, recv_sem=srecv,
             device_id={"seq": peer}, device_id_type=MESH,
         )
 
-    def send_q(i, _):
-        q_copy(me, peer_at(i)).start()
-        return 0
-
-    lax.fori_loop(0, n - 1, send_q, 0, unroll=True)
+    def await_slots(buf, count, sem):
+        some = buf.at[pl.ds(0, count)]
+        pltpu.make_async_copy(some, some, sem).wait()
+
+    for k in far_first:
+        for peer in peers_of(k):
+            q_copy(peer, k).start()
     len_load.wait()
     val_load.wait()
     for load in loads:
@@ -121,18 +129,10 @@
             parts = [op(parts[i], parts[i + 1]) for i in range(0, len(parts), 2)]
         return parts[0]
 
-    def group(gi, carry):
+    def group(k, carry):
         l0, l1, m0, m1 = carry
-        zo = (mz // 2 + zigzag(gi)) % (NZ // 2)
-        pairs = [((mx + xo) % NX) * (NZ // 2) + zo for xo in (0, 1, 3, 2)]
-        for pair in pairs:
-            for r in range(2):
-                b = 2 * pair + r
-
-                @pl.when(b != me)
-                def _():
-                    q_copy(b, b).wait_recv()
-
+        pairs = pairs_of(k)
+        await_slots(qbuf, len(peers_of(k)), qrecv.at[k])
         parts = [scores_of(pair) for pair in pairs]
         tops = [
             jnp.maximum(jnp.max(tree(jnp.maximum, ps), axis=1, keepdims=True), FLOOR) for ps in parts
@@ -158,37 +158,29 @@
                 l1 = jnp.where(skew == at - BLK, lse[rows], l1)
                 m0 = jnp.where(skew == at, top[rows], m0)
                 m1 = jnp.where(skew == at - BLK, top[rows], m1)
-        for pair in pairs:
-            for r in range(2):
-                b = 2 * pair + r
-
-                @pl.when(b != me)
-                def _():
-                    o_copy(b, me).start()
-
         return l0, l1, m0, m1
 
     zero = jnp.zeros((heads, BLK), jnp.float32)
-    l0, l1, m0, m1 = lax.fori_loop(0, NZ // 2, group, (zero, zero, zero, zero))
+    carry = (zero, zero, zero, zero)
+    for k in range(groups):
+        carry = group(k, carry)
+        if k < groups - 1:
+            for peer in peers_of(k):
+                o_copy(peer).start()
+    l0, l1, m0, m1 = carry
 
     own = jnp.concatenate([jnp.sum(l0, axis=0, keepdims=True), jnp.sum(l1, axis=0, keepdims=True)], axis=0)
     tops = jnp.concatenate([jnp.sum(m0, axis=0, keepdims=True), jnp.sum(m1, axis=0, keepdims=True)], axis=0)
     stat[...] = own
     statall[me] = own
 
-    def send_s(i, _):
-        s_copy(me, peer_at(i)).start()
-        return 0
-
-    lax.fori_loop(0, n - 1, send_s, 0, unroll=True)
+    for k in far_first:
+        for peer in peers_of(k):
+            s_copy(peer).start()
+            if k == groups - 1:
+                o_copy(peer).start()
     mixbuf[me] = obuf[me]
-
-    def take_s(i, _):
-        src = peer_at(n - 2 - i)
-        s_copy(src, src).wait_recv()
-        return 0
-
-    lax.fori_loop(0, n - 1, take_s, 0, unroll=True)
+    await_slots(statall, n - 1, srecv)
 
     every = statall[...]
     top = jnp.max(every, axis=0)
@@ -207,13 +199,7 @@
         for j in range(blocks):
             con_ref[pl.ds(r * half * blocks + j, half, stride=blocks), :] = got[:, j * BLK : (j + 1) * BLK]
 
-    def take_o(i, _):
-        src = peer_at(n - 2 - i)
-        o_copy(src, src).wait_recv()
-        return 0
-
-    lax.fori_loop(0, n - 1, take_o, 0, unroll=True)
-
+    await_slots(mixbuf, n - 1, orecv)
     my_row = me // half
     hit = skew == (me % half) * heads
     total_row = ltot[pl.ds(my_row, 1), :]
@@ -224,14 +210,9 @@
         acc = acc + part * mixbuf[d].astype(jnp.float32)
     att_ref[...] = acc
 
-    def finish(i, _):
-        peer = peer_at(i)
-        q_copy(me, peer).wait_send()
-        o_copy(peer, me).wait_send()
-        s_copy(me, peer).wait_send()
-        return 0
-
-    lax.fori_loop(0, n - 1, finish, 0, unroll=True)
+    await_slots(qbuf, n - 1, qsend)
+    await_slots(obuf, n - 1, osend)
+    await_slots(statall, n - 1, ssend)
 
 
 def closing(con_ref, att_ref, old_ref, attended_ref, heavy_ref):
@@ -271,12 +252,12 @@
             dma((4,)),
             dma((4,)),
             dma((3,)),
-            dma((n,)),
-            dma((n,)),
-            dma((n,)),
-            dma((n,)),
-            dma((n,)),
-            dma((n,)),
+            dma,
+            dma((NZ // 2,)),
+            dma,
+            dma,
+            dma,
+            dma,
         ],
         compiler_params=pltpu.CompilerParams(
             collective_id=0, has_side_effects=True, vmem_limit_bytes=16 * 2**20

time: 25.8 us -> 23.8 us (0.922)
  Pallas kernels: 25 us -> 23.1 us
    pallas_call x1, Pallas kernels: 24.4 us -> 22.5 us  [on_device(): pl.pallas_call(functools.partial(kernel, n, heads, ctx), out_shape=(jax.S...]
where the time goes in v3:
time: 23.8 us
  Pallas kernels  23.1 us (97%)
  between operations  0.66 us (3%)
    pallas_call x1, Pallas kernels, on_device(): pl.pallas_call(functools.partial(kernel, n, heads, ctx), out_shape=(jax.S...  22.5 us
    pallas_call x1, Pallas kernels, on_device(): pl.pallas_call(closing, out_shape=(jax.ShapeDtypeStruct((heads, HD), jnp....  0.64 us

profile of v3, /device:TPU:8, one launch (start us, length us, event | category | flops | bytes accessed | tf_op | source)
XLA Modules:
  0.0 23.8 jit_solution(17644592870296272907)
XLA Ops:
  0.6 0.0 copy-start
  0.6 22.5 %decode.1 = (f32[128,128]{1,0:T(8,128)S(1)}, f32[8,128]{1,0:T(8,128)S(1)}) custom-call(bf16[1,8,128]{2,1,0:T(8,128)(2,1)} %q_hbm.1, bf16[32,1,512,128]{3,2,1,0:T(8,128)(2,1)} %k_hbm.1, bf16[32,1,512,128]{3,2,1,0:T(8,128)(2,1)} %v_hbm.1, s32[32]{0:T(128)} %len_hbm.1, s32[4,32]{1,0:T(4,128)} %bitcast.5), custom_call_target="tpu_custom_call" | custom-call | tf_op jit(solution)/shard_map/decode/pallas_call | solution.py:231
  23.1 0.0 copy-done
  23.1 0.6 %closing.1 = (bf16[8,128]{1,0:T(8,128)(2,1)}, f32[128,128]{1,0:T(8,128)}) custom-call(f32[128,128]{1,0:T(8,128)S(1)} %get-tuple-element.6.con_ref, f32[8,128]{1,0:T(8,128)S(1)} %get-tuple-element.7.att_ref, f32[128,128]{1,0:T(8,128)S(1)} %bitcast.4), custom_call_target="tpu_custom_call" | custom-call | tf_op jit(solution)/shard_map/closing/pallas_call | solution.py:267
Async XLA Ops:
  0.6 22.5 %copy-start = (f32[32,1,512]{2,1,0:T(1,128)S(1)}, f32[32,1,512]{2,1,0:T(1,128)}, u32[]{:S(2)}) copy-start(f32[32,1,512]{2,1,0:T(1,128)} %param.9) | copy-start | bytes 196612

commit v4 on v3

--- a/solution.py
+++ b/solution.py
@@ -21,9 +21,9 @@
 
 
 def kernel(
-    n, heads, ctx, q_hbm, k_hbm, v_hbm, len_hbm, val_hbm, con_ref, att_ref,
-    kbuf, vbuf, kturn, qbuf, obuf, mixbuf, pbuf, stat, statall, ltot, len_s, val_s,
-    ksem, vsem, lsem, qsend, qrecv, osend, orecv, ssend, srecv,
+    n, heads, ctx, q_hbm, k_hbm, v_hbm, old_hbm, len_hbm, val_hbm, new_ref, att_ref,
+    kvbuf, old_v, kturn, qbuf, obuf, mixbuf, pbuf, ibuf, stat, statall, ltot, len_s, val_s,
+    kvsem, lsem, osem, qrecv, orecv, ssend, srecv,
 ):
     me = lax.axis_index("seq")
     mx, mz = me // NZ, me % NZ
@@ -55,11 +55,12 @@
     q_load.start()
     len_load.start()
     val_load.start()
-    loads = []
+    kbuf, vbuf = kvbuf.at[0], kvbuf.at[1]
+    loads = [pltpu.make_async_copy(old_hbm, old_v, lsem.at[3])]
     for c in range(4):
         rows = pl.ds(c * (n // 4), n // 4)
-        loads.append(pltpu.make_async_copy(k_hbm.at[rows, 0], kbuf.at[rows], ksem.at[c]))
-        loads.append(pltpu.make_async_copy(v_hbm.at[rows, 0], vbuf.at[rows], vsem.at[c]))
+        loads.append(pltpu.make_async_copy(k_hbm.at[rows, 0], kbuf.at[rows], kvsem))
+        loads.append(pltpu.make_async_copy(v_hbm.at[rows, 0], vbuf.at[rows], kvsem))
     for load in loads:
         load.start()
     q_load.wait()
@@ -67,13 +68,13 @@
 
     def q_copy(peer, k):
         return pltpu.make_async_remote_copy(
-            src_ref=qbuf.at[me], dst_ref=qbuf.at[me], send_sem=qsend, recv_sem=qrecv.at[seen_as[k]],
+            src_ref=qbuf.at[me], dst_ref=qbuf.at[me], send_sem=osem, recv_sem=qrecv.at[seen_as[k]],
             device_id={"seq": peer}, device_id_type=MESH,
         )
 
     def o_copy(b):
         return pltpu.make_async_remote_copy(
-            src_ref=obuf.at[b], dst_ref=mixbuf.at[me], send_sem=osend, recv_sem=orecv,
+            src_ref=obuf.at[b], dst_ref=mixbuf.at[me], send_sem=osem, recv_sem=orecv,
             device_id={"seq": b}, device_id_type=MESH,
         )
 
@@ -92,8 +93,8 @@
             q_copy(peer, k).start()
     len_load.wait()
     val_load.wait()
-    for load in loads:
-        load.wait()
+    loads[0].wait()
+    pltpu.make_async_copy(kvbuf, kvbuf, kvsem).wait()
 
     def turn(b, _):
         kturn[b] = kbuf[b].T
@@ -110,12 +111,15 @@
         - lax.broadcasted_iota(jnp.int32, (heads, BLK), 0)
     )
 
-    def scores_of(pair):
+    def product_of(pair):
         b0 = 2 * pair
         qp = qbuf[pl.ds(b0, 2)].astype(jnp.float32).reshape(2 * heads, HD)
         lhs = jnp.concatenate([jnp.where(upper, qp, 0.0), jnp.where(upper, 0.0, qp)], axis=1).astype(jnp.bfloat16)
         keys = jnp.concatenate([kturn[b0], kturn[b0 + 1]], axis=0)
-        s = jnp.dot(lhs, keys, preferred_element_type=jnp.float32)
+        return jnp.dot(lhs, keys, preferred_element_type=jnp.float32)
+
+    def masked(pair, s):
+        b0 = 2 * pair
         s = s * HD ** (-0.5)
         parts = []
         for j in range(blocks):
@@ -129,11 +133,14 @@
             parts = [op(parts[i], parts[i + 1]) for i in range(0, len(parts), 2)]
         return parts[0]
 
-    def group(k, carry):
+    def products(k):
+        await_slots(qbuf, len(peers_of(k)), qrecv.at[k])
+        return [product_of(pair) for pair in pairs_of(k)]
+
+    def weigh(k, raw, carry):
         l0, l1, m0, m1 = carry
         pairs = pairs_of(k)
-        await_slots(qbuf, len(peers_of(k)), qrecv.at[k])
-        parts = [scores_of(pair) for pair in pairs]
+        parts = [masked(pair, s) for pair, s in zip(pairs, raw)]
         tops = [
             jnp.maximum(jnp.max(tree(jnp.maximum, ps), axis=1, keepdims=True), FLOOR) for ps in parts
         ]
@@ -141,45 +148,69 @@
         totals = [
             jnp.maximum(jnp.sum(tree(jnp.add, es), axis=1, keepdims=True), TINY) for es in expos
         ]
+        weights = []
         for pair, top, es, total in zip(pairs, tops, expos, totals):
-            b0 = 2 * pair
             w = jnp.concatenate(es, axis=1).astype(jnp.bfloat16)
+            weights.append(w)
             pbuf[pl.ds(pl.multiple_of(pair * 2 * heads, 2 * heads), 2 * heads), :] = w
-            vals = jnp.concatenate([vbuf[b0], vbuf[b0 + 1]], axis=1)
-            mixed = jnp.dot(w, vals, preferred_element_type=jnp.float32)
-            inv = 1.0 / total
+            ibuf[pair] = jnp.broadcast_to(1.0 / total, (2 * heads, HD))
             lse = top + jnp.log(total)
             for r in range(2):
                 rows = slice(r * heads, (r + 1) * heads)
-                part = mixed[rows, r * HD : (r + 1) * HD] * inv[rows]
-                obuf[b0 + r] = part.astype(jnp.bfloat16)
-                at = (b0 + r) * heads
+                at = (2 * pair + r) * heads
                 l0 = jnp.where(skew == at, lse[rows], l0)
                 l1 = jnp.where(skew == at - BLK, lse[rows], l1)
                 m0 = jnp.where(skew == at, top[rows], m0)
                 m1 = jnp.where(skew == at - BLK, top[rows], m1)
-        return l0, l1, m0, m1
+        return (l0, l1, m0, m1), weights
+
+    def mixed_of(pair, w):
+        vals = jnp.concatenate([vbuf[2 * pair], vbuf[2 * pair + 1]], axis=1)
+        return jnp.dot(w, vals, preferred_element_type=jnp.float32)
+
+    def keep(pair, mixed):
+        inv = ibuf[pair]
+        for r in range(2):
+            rows = slice(r * heads, (r + 1) * heads)
+            obuf[2 * pair + r] = (mixed[rows, r * HD : (r + 1) * HD] * inv[rows]).astype(jnp.bfloat16)
+
+    def mix(k):
+        for pair in pairs_of(k):
+            keep(pair, mixed_of(pair, pbuf[pl.ds(pl.multiple_of(pair * 2 * heads, 2 * heads), 2 * heads), :]))
 
     zero = jnp.zeros((heads, BLK), jnp.float32)
     carry = (zero, zero, zero, zero)
-    for k in range(groups):
-        carry = group(k, carry)
-        if k < groups - 1:
-            for peer in peers_of(k):
-                o_copy(peer).start()
-    l0, l1, m0, m1 = carry
+    raw = products(0)
+    for k in range(1, groups):
+        later = products(k)
+        carry, _ = weigh(k - 1, raw, carry)
+        raw = later
+    last = groups - 1
+    (l0, l1, m0, m1), weights = weigh(last, raw, carry)
+    mixed = [mixed_of(pair, w) for pair, w in zip(pairs_of(last), weights)]
 
     own = jnp.concatenate([jnp.sum(l0, axis=0, keepdims=True), jnp.sum(l1, axis=0, keepdims=True)], axis=0)
     tops = jnp.concatenate([jnp.sum(m0, axis=0, keepdims=True), jnp.sum(m1, axis=0, keepdims=True)], axis=0)
     stat[...] = own
     statall[me] = own
 
-    for k in far_first:
+    for peer in peers_of(last):
+        s_copy(peer).start()
+    for pair, product in zip(pairs_of(last), mixed):
+        keep(pair, product)
+    for peer in peers_of(last):
+        o_copy(peer).start()
+    for k in far_first[1:]:
         for peer in peers_of(k):
             s_copy(peer).start()
-            if k == groups - 1:
+    for k in far_first[1:]:
+        mix(k)
+        if k + 1 < last:
+            for peer in peers_of(k + 1):
                 o_copy(peer).start()
     mixbuf[me] = obuf[me]
+    for peer in peers_of(0):
+        o_copy(peer).start()
     await_slots(statall, n - 1, srecv)
 
     every = statall[...]
@@ -197,27 +228,30 @@
         got = jnp.dot(both, pbuf[r * BLK : (r + 1) * BLK, :], preferred_element_type=jnp.float32)
         got = got[:half] + got[half:]
         for j in range(blocks):
-            con_ref[pl.ds(r * half * blocks + j, half, stride=blocks), :] = got[:, j * BLK : (j + 1) * BLK]
-
-    await_slots(mixbuf, n - 1, orecv)
+            at = pl.ds(r * half * blocks + j, half, stride=blocks)
+            new_ref[at, :] = old_v[at, :] + got[:, j * BLK : (j + 1) * BLK]
+
     my_row = me // half
     hit = skew == (me % half) * heads
     total_row = ltot[pl.ds(my_row, 1), :]
+    factors = []
+    for d in range(n):
+        gap = jnp.broadcast_to(statall[d, pl.ds(my_row, 1), :] - total_row, (heads, BLK))
+        factors.append(jnp.exp(jnp.sum(jnp.where(hit, gap, 0.0), axis=1, keepdims=True)))
+    await_slots(mixbuf, n - 1, orecv)
     acc = zero
     for d in range(n):
-        gap = jnp.broadcast_to(statall[d, pl.ds(my_row, 1), :] - total_row, (heads, BLK))
-        part = jnp.exp(jnp.sum(jnp.where(hit, gap, 0.0), axis=1, keepdims=True))
-        acc = acc + part * mixbuf[d].astype(jnp.float32)
+        acc = acc + factors[d] * mixbuf[d].astype(jnp.float32)
     att_ref[...] = acc
 
-    await_slots(qbuf, n - 1, qsend)
-    await_slots(obuf, n - 1, osend)
+    both = kbuf.at[0, pl.ds(0, 2 * (n - 1) * heads)]
+    pltpu.make_async_copy(both, both, osem).wait()
     await_slots(statall, n - 1, ssend)
 
 
-def closing(con_ref, att_ref, old_ref, attended_ref, heavy_ref):
+def closing(new_ref, att_ref, heavy_ref, attended_ref):
+    heavy_ref[...] = new_ref[...]
     attended_ref[...] = att_ref[...].astype(jnp.bfloat16)
-    heavy_ref[...] = old_ref[...] + con_ref[...]
 
 
 def on_device(queries, keys, values, old_scores, lengths, valid_counts):
@@ -228,33 +262,32 @@
     anywhere = pl.BlockSpec(memory_space=pltpu.HBM)
     vmem = pl.BlockSpec(memory_space=pltpu.VMEM)
     dma = pltpu.SemaphoreType.DMA
-    added, attended = pl.pallas_call(
+    updated, mixed = pl.pallas_call(
         functools.partial(kernel, n, heads, ctx),
         out_shape=(
             jax.ShapeDtypeStruct((n * blocks, BLK), jnp.float32),
             jax.ShapeDtypeStruct((heads, HD), jnp.float32),
         ),
-        in_specs=[anywhere] * 5,
+        in_specs=[anywhere] * 6,
         out_specs=(vmem, vmem),
         scratch_shapes=[
-            pltpu.VMEM((n, ctx, HD), jnp.bfloat16),
-            pltpu.VMEM((n, ctx, HD), jnp.bfloat16),
+            pltpu.VMEM((2, n, ctx, HD), jnp.bfloat16),
+            pltpu.VMEM((n * blocks, BLK), jnp.float32),
             pltpu.VMEM((n, HD, ctx), jnp.bfloat16),
             pltpu.VMEM((n, heads, HD), jnp.bfloat16),
             pltpu.VMEM((n, heads, HD), jnp.bfloat16),
             pltpu.VMEM((n, heads, HD), jnp.bfloat16),
             pltpu.VMEM((n * heads, ctx), jnp.bfloat16),
+            pltpu.VMEM((n // 2, 2 * heads, HD), jnp.float32),
             pltpu.VMEM((2, BLK), jnp.float32),
             pltpu.VMEM((n, 2, BLK), jnp.float32),
             pltpu.VMEM((2, BLK), jnp.float32),
             pltpu.SMEM((n,), jnp.int32),
             pltpu.SMEM((blocks, n), jnp.int32),
+            dma,
             dma((4,)),
-            dma((4,)),
-            dma((3,)),
             dma,
             dma((NZ // 2,)),
-            dma,
             dma,
             dma,
             dma,
@@ -263,18 +296,23 @@
             collective_id=0, has_side_effects=True, vmem_limit_bytes=16 * 2**20
         ),
         name="decode",
-    )(*(pltpu.with_memory_space_constraint(a, pltpu.HBM) for a in (queries, keys, values, lengths, valid_counts.T)))
-    attended, heavy = pl.pallas_call(
+    )(
+        *(
+            pltpu.with_memory_space_constraint(a, pltpu.HBM)
+            for a in (queries, keys, values, old_scores.reshape(n * blocks, BLK), lengths, valid_counts.T)
+        )
+    )
+    heavy, attended = pl.pallas_call(
         closing,
         out_shape=(
+            jax.ShapeDtypeStruct((n * blocks, BLK), jnp.float32),
             jax.ShapeDtypeStruct((heads, HD), jnp.bfloat16),
-            jax.ShapeDtypeStruct((n * blocks, BLK), jnp.float32),
         ),
-        in_specs=[vmem] * 3,
+        in_specs=[vmem] * 2,
         out_specs=(vmem, vmem),
         compiler_params=pltpu.CompilerParams(vmem_limit_bytes=2**20),
         name="closing",
-    )(added, attended, old_scores.reshape(n * blocks, BLK))
+    )(updated, mixed)
     return attended[None], heavy.reshape(old_scores.shape)
 
 

time: 23.8 us -> 23.5 us (0.987)
  Pallas kernels: 23.1 us -> 22.8 us
    pallas_call x1, Pallas kernels: 22.5 us -> 22.2 us  [on_device(): pl.pallas_call(functools.partial(kernel, n, heads, ctx), out_shape=(jax.S...]
where the time goes in v4:
time: 23.5 us; the launch traced here: 23.4 us
  Pallas kernels  22.8 us (97%)
  between operations  0.64 us (3%)
    pallas_call x1, Pallas kernels, on_device(): pl.pallas_call(functools.partial(kernel, n, heads, ctx), out_shape=(jax.S...  22.2 us
    pallas_call x1, Pallas kernels, on_device(): pl.pallas_call(closing, out_shape=(jax.ShapeDtypeStruct((n * blocks, BLK)...  0.64 us

profile of v4, /device:TPU:8, one launch (start us, length us, event | category | flops | bytes accessed | tf_op | source)
XLA Modules:
  0.0 23.4 jit_solution(2139390245061093026)
XLA Ops:
  0.6 22.2 %decode.1 = (f32[128,128]{1,0:T(8,128)S(1)}, f32[8,128]{1,0:T(8,128)S(1)}) custom-call(bf16[1,8,128]{2,1,0:T(8,128)(2,1)} %q_hbm.1, bf16[32,1,512,128]{3,2,1,0:T(8,128)(2,1)} %k_hbm.1, bf16[32,1,512,128]{3,2,1,0:T(8,128)(2,1)} %v_hbm.1, f32[128,128]{1,0:T(8,128)} %bitcast.4, s32[32]{0:T(128)} %len_hbm.1, s32[4,32]{1,0:T(4,128)} %bitcast.5), custom_call_target="tpu_custom_call" | custom-call | tf_op jit(solution)/shard_map/decode/pallas_call | solution.py:265
  22.8 0.6 %closing.1 = (f32[128,128]{1,0:T(8,128)}, bf16[8,128]{1,0:T(8,128)(2,1)}) custom-call(f32[128,128]{1,0:T(8,128)S(1)} %get-tuple-element.6.new_ref, f32[8,128]{1,0:T(8,128)S(1)} %get-tuple-element.7.att_ref), custom_call_target="tpu_custom_call" | custom-call | tf_op jit(solution)/shard_map/closing/pallas_call | solution.py:305

commit v5 on v4

--- a/solution.py
+++ b/solution.py
@@ -16,13 +16,9 @@
 MESH = pl.DeviceIdType.MESH
 
 
-def zigzag(k):
-    return ((k + 1) // 2) * (2 * (k % 2) - 1)
-
-
 def kernel(
     n, heads, ctx, q_hbm, k_hbm, v_hbm, old_hbm, len_hbm, val_hbm, new_ref, att_ref,
-    kvbuf, old_v, kturn, qbuf, obuf, mixbuf, pbuf, ibuf, stat, statall, ltot, len_s, val_s,
+    kvbuf, old_v, kturn, qbuf, obuf, mixbuf, spare, pbuf, ibuf, stat, statall, ltot, len_s, val_s,
     kvsem, lsem, osem, qrecv, orecv, ssend, srecv,
 ):
     me = lax.axis_index("seq")
@@ -30,29 +26,35 @@
     blocks = ctx // BLK
     half = n // 2
 
-    def pairs_of(k):
-        zo = (mz // 2 + zigzag(k)) % (NZ // 2)
-        return [((mx + xo) % NX) * (NZ // 2) + zo for xo in (0, 1, 3, 2)]
-
-    def peers_of(k):
-        found = []
-        for pair in pairs_of(k)[::-1]:
-            found += [2 * pair, 2 * pair + 1]
-        return found[:-2] + [me + 1 - 2 * (me % 2)] if k == 0 else found
-
-    groups = NZ // 2
-    far_first = list(range(groups))[::-1]
-    seen_as = (0, 2, 1, 3)
+    places = NZ // 2
+    mzo = mz // 2
+
+    def pairs_of(zo):
+        return [((mx + xo) % NX) * places + zo for xo in (2, 1, 3, 0)]
+
+    def for_peers(zo, act, act_far=None):
+        for i, pair in enumerate(pairs_of(zo)):
+            for b in (2 * pair, 2 * pair + 1):
+                if i == 0 and act_far is not None:
+                    act_far(b)
+                elif i < NX - 1:
+                    act(b)
+                else:
+                    pl.when(b != me)(functools.partial(act, b))
 
     barrier = pltpu.get_barrier_semaphore()
-    for k in far_first:
-        for peer in peers_of(k):
-            pl.semaphore_signal(barrier, inc=1, device_id={"seq": peer}, device_id_type=MESH)
+
+    def greet(peer):
+        pl.semaphore_signal(barrier, inc=1, device_id={"seq": peer}, device_id_type=MESH)
+
+    for zo in range(places):
+        for_peers(zo, greet)
 
     q_load = pltpu.make_async_copy(q_hbm.at[0], qbuf.at[me], lsem.at[0])
     len_load = pltpu.make_async_copy(len_hbm, len_s, lsem.at[1])
     val_load = pltpu.make_async_copy(val_hbm, val_s, lsem.at[2])
     q_load.start()
+    pltpu.make_async_copy(q_hbm.at[0], spare, qrecv.at[mzo]).start()
     len_load.start()
     val_load.start()
     kbuf, vbuf = kvbuf.at[0], kvbuf.at[1]
@@ -66,31 +68,32 @@
     q_load.wait()
     pl.semaphore_wait(barrier, n - 1)
 
-    def q_copy(peer, k):
-        return pltpu.make_async_remote_copy(
-            src_ref=qbuf.at[me], dst_ref=qbuf.at[me], send_sem=osem, recv_sem=qrecv.at[seen_as[k]],
+    far_sem = mzo + places * (1 - (mzo + places - 1) // places)
+
+    def send_q(sem, peer):
+        pltpu.make_async_remote_copy(
+            src_ref=qbuf.at[me], dst_ref=qbuf.at[me], send_sem=osem, recv_sem=qrecv.at[sem],
             device_id={"seq": peer}, device_id_type=MESH,
-        )
-
-    def o_copy(b):
-        return pltpu.make_async_remote_copy(
+        ).start()
+
+    def send_o(b):
+        pltpu.make_async_remote_copy(
             src_ref=obuf.at[b], dst_ref=mixbuf.at[me], send_sem=osem, recv_sem=orecv,
             device_id={"seq": b}, device_id_type=MESH,
-        )
-
-    def s_copy(peer):
-        return pltpu.make_async_remote_copy(
+        ).start()
+
+    def send_s(peer):
+        pltpu.make_async_remote_copy(
             src_ref=stat, dst_ref=statall.at[me], send_sem=ssend, recv_sem=srecv,
             device_id={"seq": peer}, device_id_type=MESH,
-        )
+        ).start()
 
     def await_slots(buf, count, sem):
         some = buf.at[pl.ds(0, count)]
         pltpu.make_async_copy(some, some, sem).wait()
 
-    for k in far_first:
-        for peer in peers_of(k):
-            q_copy(peer, k).start()
+    for zo in (2, 3, 1, 0):
+        for_peers(zo, functools.partial(send_q, mzo), functools.partial(send_q, far_sem))
     len_load.wait()
     val_load.wait()
     loads[0].wait()
@@ -133,13 +136,14 @@
             parts = [op(parts[i], parts[i + 1]) for i in range(0, len(parts), 2)]
         return parts[0]
 
-    def products(k):
-        await_slots(qbuf, len(peers_of(k)), qrecv.at[k])
-        return [product_of(pair) for pair in pairs_of(k)]
-
-    def weigh(k, raw, carry):
+    def products(k, some=slice(None)):
+        pairs = pairs_of(k)[some]
+        at = places if k == 0 and some == slice(0, 1) else k
+        await_slots(qbuf, 2 * len(pairs), qrecv.at[at])
+        return [product_of(pair) for pair in pairs]
+
+    def weigh(pairs, raw, carry):
         l0, l1, m0, m1 = carry
-        pairs = pairs_of(k)
         parts = [masked(pair, s) for pair, s in zip(pairs, raw)]
         tops = [
             jnp.maximum(jnp.max(tree(jnp.maximum, ps), axis=1, keepdims=True), FLOOR) for ps in parts
@@ -180,37 +184,35 @@
 
     zero = jnp.zeros((heads, BLK), jnp.float32)
     carry = (zero, zero, zero, zero)
-    raw = products(0)
-    for k in range(1, groups):
-        later = products(k)
-        carry, _ = weigh(k - 1, raw, carry)
+    order = [(k, slice(None)) for k in range(places)[:0:-1]] + [(0, slice(1, None)), (0, slice(0, 1))]
+    raw = products(*order[0])
+    kept = []
+    for (before, some), now in zip(order, order[1:]):
+        later = products(*now)
+        carry, kept = weigh(pairs_of(before)[some], raw, carry)
         raw = later
-    last = groups - 1
-    (l0, l1, m0, m1), weights = weigh(last, raw, carry)
-    mixed = [mixed_of(pair, w) for pair, w in zip(pairs_of(last), weights)]
+    (l0, l1, m0, m1), weights = weigh(pairs_of(0)[:1], raw, carry)
+    weights = weights + kept
+    mixed = [mixed_of(pair, w) for pair, w in zip(pairs_of(0), weights)]
 
     own = jnp.concatenate([jnp.sum(l0, axis=0, keepdims=True), jnp.sum(l1, axis=0, keepdims=True)], axis=0)
     tops = jnp.concatenate([jnp.sum(m0, axis=0, keepdims=True), jnp.sum(m1, axis=0, keepdims=True)], axis=0)
     stat[...] = own
     statall[me] = own
 
-    for peer in peers_of(last):
-        s_copy(peer).start()
-    for pair, product in zip(pairs_of(last), mixed):
+    for_peers(0, send_s)
+    for pair, product in zip(pairs_of(0), mixed):
         keep(pair, product)
-    for peer in peers_of(last):
-        o_copy(peer).start()
-    for k in far_first[1:]:
-        for peer in peers_of(k):
-            s_copy(peer).start()
-    for k in far_first[1:]:
-        mix(k)
-        if k + 1 < last:
-            for peer in peers_of(k + 1):
-                o_copy(peer).start()
+    for_peers(0, send_o)
+    for_peers(1, send_s)
+    mix(1)
+    for_peers(1, send_o)
+    for_peers(2, send_s)
+    for_peers(3, send_s)
+    for zo in (2, 3):
+        mix(zo)
+        for_peers(zo, send_o)
     mixbuf[me] = obuf[me]
-    for peer in peers_of(0):
-        o_copy(peer).start()
     await_slots(statall, n - 1, srecv)
 
     every = statall[...]
@@ -277,6 +279,7 @@
             pltpu.VMEM((n, heads, HD), jnp.bfloat16),
             pltpu.VMEM((n, heads, HD), jnp.bfloat16),
             pltpu.VMEM((n, heads, HD), jnp.bfloat16),
+            pltpu.VMEM((heads, HD), jnp.bfloat16),
             pltpu.VMEM((n * heads, ctx), jnp.bfloat16),
             pltpu.VMEM((n // 2, 2 * heads, HD), jnp.float32),
             pltpu.VMEM((2, BLK), jnp.float32),
@@ -287,7 +290,7 @@
             dma,
             dma((4,)),
             dma,
-            dma((NZ // 2,)),
+            dma((NZ // 2 + 1,)),
             dma,
             dma,
             dma,

time: 23.5 us -> 23.4 us (level)
  no operation moved by 1% of the time
where the time goes in v5:
time: 23.4 us; the launch traced here: 23.3 us
  Pallas kernels  22.7 us (97%)
  between operations  0.64 us (3%)
    pallas_call x1, Pallas kernels, on_device(): pl.pallas_call(functools.partial(kernel, n, heads, ctx), out_shape=(jax.S...  22 us
    pallas_call x1, Pallas kernels, on_device(): pl.pallas_call(closing, out_shape=(jax.ShapeDtypeStruct((n * blocks, BLK)...  0.64 us

profile of v5, /device:TPU:8, one launch (start us, length us, event | category | flops | bytes accessed | tf_op | source)
XLA Modules:
  0.0 23.3 jit_solution(14301511101992682641)
XLA Ops:
  0.6 22.0 %decode.1 = (f32[128,128]{1,0:T(8,128)S(1)}, f32[8,128]{1,0:T(8,128)S(1)}) custom-call(bf16[1,8,128]{2,1,0:T(8,128)(2,1)} %q_hbm.1, bf16[32,1,512,128]{3,2,1,0:T(8,128)(2,1)} %k_hbm.1, bf16[32,1,512,128]{3,2,1,0:T(8,128)(2,1)} %v_hbm.1, f32[128,128]{1,0:T(8,128)} %bitcast.4, s32[32]{0:T(128)} %len_hbm.1, s32[4,32]{1,0:T(4,128)} %bitcast.5), custom_call_target="tpu_custom_call" | custom-call | tf_op jit(solution)/shard_map/decode/pallas_call | solution.py:267
  22.7 0.6 %closing.1 = (f32[128,128]{1,0:T(8,128)}, bf16[8,128]{1,0:T(8,128)(2,1)}) custom-call(f32[128,128]{1,0:T(8,128)S(1)} %get-tuple-element.6.new_ref, f32[8,128]{1,0:T(8,128)S(1)} %get-tuple-element.7.att_ref), custom_call_target="tpu_custom_call" | custom-call | tf_op jit(solution)/shard_map/closing/pallas_call | solution.py:308

commit v6 on v5

--- a/solution.py
+++ b/solution.py
@@ -19,7 +19,7 @@
 def kernel(
     n, heads, ctx, q_hbm, k_hbm, v_hbm, old_hbm, len_hbm, val_hbm, new_ref, att_ref,
     kvbuf, old_v, kturn, qbuf, obuf, mixbuf, spare, pbuf, ibuf, stat, statall, ltot, len_s, val_s,
-    kvsem, lsem, osem, qrecv, orecv, ssend, srecv,
+    kvsem, lsem, qsend, osem, qrecv, orecv, ssend, srecv,
 ):
     me = lax.axis_index("seq")
     mx, mz = me // NZ, me % NZ
@@ -72,7 +72,7 @@
 
     def send_q(sem, peer):
         pltpu.make_async_remote_copy(
-            src_ref=qbuf.at[me], dst_ref=qbuf.at[me], send_sem=osem, recv_sem=qrecv.at[sem],
+            src_ref=qbuf.at[me], dst_ref=qbuf.at[me], send_sem=qsend, recv_sem=qrecv.at[sem],
             device_id={"seq": peer}, device_id_type=MESH,
         ).start()
 
@@ -176,7 +176,7 @@
         inv = ibuf[pair]
         for r in range(2):
             rows = slice(r * heads, (r + 1) * heads)
-            obuf[2 * pair + r] = (mixed[rows, r * HD : (r + 1) * HD] * inv[rows]).astype(jnp.bfloat16)
+            obuf[2 * pair + r] = mixed[rows, r * HD : (r + 1) * HD] * inv[rows]
 
     def mix(k):
         for pair in pairs_of(k):
@@ -243,11 +243,11 @@
     await_slots(mixbuf, n - 1, orecv)
     acc = zero
     for d in range(n):
-        acc = acc + factors[d] * mixbuf[d].astype(jnp.float32)
+        acc = acc + factors[d] * mixbuf[d]
     att_ref[...] = acc
 
-    both = kbuf.at[0, pl.ds(0, 2 * (n - 1) * heads)]
-    pltpu.make_async_copy(both, both, osem).wait()
+    await_slots(qbuf, n - 1, qsend)
+    await_slots(obuf, n - 1, osem)
     await_slots(statall, n - 1, ssend)
 
 
@@ -277,8 +277,8 @@
             pltpu.VMEM((n * blocks, BLK), jnp.float32),
             pltpu.VMEM((n, HD, ctx), jnp.bfloat16),
             pltpu.VMEM((n, heads, HD), jnp.bfloat16),
-            pltpu.VMEM((n, heads, HD), jnp.bfloat16),
-            pltpu.VMEM((n, heads, HD), jnp.bfloat16),
+            pltpu.VMEM((n, heads, HD), jnp.float32),
+            pltpu.VMEM((n, heads, HD), jnp.float32),
             pltpu.VMEM((heads, HD), jnp.bfloat16),
             pltpu.VMEM((n * heads, ctx), jnp.bfloat16),
             pltpu.VMEM((n // 2, 2 * heads, HD), jnp.float32),
@@ -289,6 +289,7 @@
             pltpu.SMEM((blocks, n), jnp.int32),
             dma,
             dma((4,)),
+            dma,
             dma,
             dma((NZ // 2 + 1,)),
             dma,

time: 23.4 us -> 23.5 us (level)
  no operation moved by 1% of the time
where the time goes in v6:
time: 23.5 us; the launch traced here: 23.4 us
  Pallas kernels  22.7 us (97%)
  between operations  0.64 us (3%)
    pallas_call x1, Pallas kernels, on_device(): pl.pallas_call(functools.partial(kernel, n, heads, ctx), out_shape=(jax.S...  22.1 us
    pallas_call x1, Pallas kernels, on_device(): pl.pallas_call(closing, out_shape=(jax.ShapeDtypeStruct((n * blocks, BLK)...  0.64 us

profile of v6, /device:TPU:8, one launch (start us, length us, event | category | flops | bytes accessed | tf_op | source)
XLA Modules:
  0.0 23.4 jit_solution(13733596665761934439)
XLA Ops:
  0.6 22.1 %decode.1 = (f32[128,128]{1,0:T(8,128)S(1)}, f32[8,128]{1,0:T(8,128)S(1)}) custom-call(bf16[1,8,128]{2,1,0:T(8,128)(2,1)} %q_hbm.1, bf16[32,1,512,128]{3,2,1,0:T(8,128)(2,1)} %k_hbm.1, bf16[32,1,512,128]{3,2,1,0:T(8,128)(2,1)} %v_hbm.1, f32[128,128]{1,0:T(8,128)} %bitcast.4, s32[32]{0:T(128)} %len_hbm.1, s32[4,32]{1,0:T(4,128)} %bitcast.5), custom_call_target="tpu_custom_call" | custom-call | tf_op jit(solution)/shard_map/decode/pallas_call | solution.py:267
  22.7 0.6 %closing.1 = (f32[128,128]{1,0:T(8,128)}, bf16[8,128]{1,0:T(8,128)(2,1)}) custom-call(f32[128,128]{1,0:T(8,128)S(1)} %get-tuple-element.6.new_ref, f32[8,128]{1,0:T(8,128)S(1)} %get-tuple-element.7.att_ref), custom_call_target="tpu_custom_call" | custom-call | tf_op jit(solution)/shard_map/closing/pallas_call | solution.py:309
